TPU v7x, 32 devices: a whole 2x2x4 slice. The times are simulated.
32 devices in a mesh: dp: 4 (over x, core), param: 8 (over z, y).
Axes of the slice: x: 2, y: 2, z: 4, core: 2. Of those that a mesh axis runs over, the one named last changes fastest.
Arguments:
- train_grads: bfloat16 [3584, 212992], P('dp', 'param'), as said below
- query_grads: bfloat16 [128, 212992], P('dp', 'param'), as said below
Outputs:
- scores: float32 [128, 3584], P('param', 'dp')
Inputs may be any that keep to these rules, and one draw needn't show every extreme that they name: `train_grads`: finite real values. `query_grads`: finite real values.
All inputs are finite; a program needn't handle non-finite values.
Results may differ from a plain program's by a relative error of at most 0.0003.
Values may be sent and summed in bfloat16 or wider, within the bound.
A program may use at most 128 MiB of HBM per device.

v0:
```python
import jax
import jax.numpy as jnp
from jax import lax
from jax.sharding import PartitionSpec as P

epsilon = 1e-06


def per_device(train_grads, query_grads):
    queries = lax.all_gather(query_grads, "dp", axis=0, tiled=True)
    products = lax.dot_general(
        queries, train_grads, (((1,), (1,)), ((), ())), preferred_element_type=jnp.float32
    )
    query_norm = jnp.sum(jnp.square(queries.astype(jnp.float32)), axis=1)
    train_norm = jnp.sum(jnp.square(train_grads.astype(jnp.float32)), axis=1)
    products, query_norm = (
        lax.psum_scatter(products, "param", scatter_dimension=0, tiled=True),
        lax.psum_scatter(query_norm, "param", scatter_dimension=0, tiled=True),
    )
    train_norm = lax.psum(train_norm, "param")
    return (
        products
        * lax.rsqrt(query_norm + epsilon)[:, None]
        * lax.rsqrt(train_norm + epsilon)[None, :]
    )


def solution(mesh):
    return jax.shard_map(
        per_device,
        mesh=mesh,
        in_specs=(P("dp", "param"), P("dp", "param")),
        out_specs=P("param", "dp"),
        check_vma=False,
    )
```

profile of v0, /device:TPU:6, one launch (start us, length us, event | category | flops | bytes accessed | tf_op | source)
XLA Modules:
  0.0 152.9 jit_solution(13825321456841834263)
XLA Ops:
  6.5 0.0 all-gather.2.cloned.1.call-start
  6.5 0.7 all-gather.2.cloned.1.call-update
  7.3 0.0 reduce-scatter.2.cloned.1.call-start
  7.3 51.2 %all-gather.2.cloned.1.call-done = bf16[128,26624]{1,0:T(8,128)(2,1)} async-done(((bf16[32,26624]{1,0:T(8,128)(2,1)}), bf16[128,26624]{1,0:T(8,128)(2,1)}) %all-gather.2.cloned.1.call-update) | async-done | bytes 6815760 | tf_op jit(solution)/shard_map/all_gather | solution.py:10
  58.5 22.4 %fusion.1 = f32[128,896]{1,0:T(8,128)} fusion(bf16[128,26624]{1,0:T(8,128)(2,1)} %all-gather.2.cloned.1.call-done, bf16[896,26624]{1,0:T(8,128)(2,1)} %param.2), kind=kOutput, calls=%fused_computation.6 | convolution fusion | flops 6106906624 | bytes 54984704 | tf_op jit(solution)/shard_map/dot_general | solution.py:11
  81.0 0.0 reduce-scatter.2.cloned.1.call-update
  81.0 0.0 copy-start
  81.0 16.4 %multiply_reduce_fusion = f32[896]{0:T(1024)S(1)} fusion(bf16[896,26624]{1,0:T(8,128)(2,1)} %param.2), kind=kLoop, calls=%fused_computation | loop fusion | flops 71564416 | bytes 47713792 | tf_op jit(solution)/shard_map/reduce_sum | solution.py:15
  97.4 0.0 copy-done
  97.4 0.6 dynamic-slice
  98.6 4.4 %multiply_reduce_fusion.1 = f32[128]{0:T(128)S(1)} fusion(bf16[128,26624]{1,0:T(8,128)(2,1)} %all-gather.2.cloned.1.call-done), kind=kLoop, calls=%fused_computation.1 | loop fusion | flops 10223488 | bytes 6816256 | tf_op jit(solution)/shard_map/reduce_sum | solution.py:14
  103.0 18.0 %all-reduce.1 = (f32[896]{0:T(1024)S(1)}, f32[128]{0:T(128)S(1)}) all-reduce(f32[896]{0:T(1024)S(1)} %multiply_reduce_fusion, f32[128]{0:T(128)S(1)} %multiply_reduce_fusion.1), channel_id=1, replica_groups=mesh['dp'=4,'param'=8] {'param'}, use_global_device_ids=true, to_apply=%region_4.0 | all-reduce | flops 1024 | bytes 8192 | tf_op jit(solution)/shard_map/psum | solution.py:20
  121.0 0.1 fusion
  121.1 23.4 %reduce-scatter.2.cloned.1.call-done = f32[16,896]{1,0:T(8,128)} async-done(((f32[128,896]{1,0:T(8,128)}), f32[16,896]{1,0:T(8,128)}) %reduce-scatter.2.cloned.1.call-update) | async-done | bytes 57360 | tf_op jit(solution)/shard_map/reduce_scatter | solution.py:17
  144.5 1.5 multiply_multiply_fusion
  (1 shorter events, 0.0 us)
Async XLA Ops:
  6.5 52.0 %all-gather.2.cloned.1.call-start = ((), (), s32[]{:S(2)}) async-start(), calls=%async_computation.1 | async-start | bytes 8519680 | tf_op jit(solution)/shard_map/all_gather | solution.py:10
  7.3 137.3 %reduce-scatter.2.cloned.1.call-start = ((), (), s32[]{:S(2)}) async-start(), calls=%async_computation.2 | async-start | bytes 516096 | tf_op jit(solution)/shard_map/reduce_scatter | solution.py:17
  81.0 16.4 %copy-start = (u32[32]{0:T(128)S(1)}, u32[32]{0:T(128)}, u32[]{:S(2)}) copy-start(u32[32]{0:T(128)} %constant.7) | copy-start | bytes 388
Sparse Core Ops, SparseCore 0:
  8.9 49.5 all-gather.1
  81.1 63.3 reduce-scatter.1
where the time goes:
time: 155 us; the launch traced here: 153 us
  waiting for transfers between devices  75.3 us (49%)
  matrix products  22.4 us (14%)
  other arithmetic  22.3 us (14%)
  blocking collectives  18 us (12%)
  between operations  14.1 us (9%)
    all_gather x1, waiting for transfers between devices, per_device(): queries = lax.all_gather(query_grads, 'dp', axis=0, tiled=True)  51.2 us
    reduce_scatter x1, waiting for transfers between devices, per_device(): lax.psum_scatter(products, 'param', scatter_dimension=0, tiled=True)  23.4 us
    dot_general x1, matrix products, per_device(): lax.dot_general(queries, train_grads, (((1,), (1,)), ((), ())), preferred...  22.4 us
    psum x1, blocking collectives, per_device(): train_norm = lax.psum(train_norm, 'param')  18 us
    reduce_sum x1, other arithmetic, per_device(): train_norm = jnp.sum(jnp.square(train_grads.astype(jnp.float32)), axis=1)  16.4 us
    reduce_sum x1, other arithmetic, per_device(): query_norm = jnp.sum(jnp.square(queries.astype(jnp.float32)), axis=1)  4.36 us
  transfers between devices with their start and end apart: 2, of which 2 were waited for; matrix products, arithmetic and copies ran while one was open for 14% of the time, Pallas kernels for 0%

commit v1 on v0

v1 whole, which is shorter than its diff:
```python
import functools

import jax
import jax.numpy as jnp
from jax import lax
from jax.experimental import pallas as pl
from jax.experimental.pallas import tpu as pltpu
from jax.sharding import PartitionSpec as P

epsilon = 1e-06
lanes = 128
max_chunk = 2048
ahead = 2
block_rows = 256


def chunk_width(width):
    best = lanes
    for tiles in range(1, max_chunk // lanes + 1):
        if width % (tiles * lanes) == 0:
            best = tiles * lanes
    return best


def nt_dot(a, b):
    return lax.dot_general(a, b, (((1,), (1,)), ((), ())), preferred_element_type=jnp.float32)


def kernel(
    cfg, train_hbm, query_hbm, out_ref,
    train, first_q, second_q, first_sum, second_sum, norm_sum, parts, norm_parts,
    train_sem, self_sem, x_send, x_recv, mate_send, mate_recv, fwd_send, fwd_recv,
    part_send, part_recv, norm_send, norm_recv,
):
    chips, params, chunks, width, rows, unit, count, owned, piece = cfg
    dp = lax.axis_index("dp")
    me = lax.axis_index("param")
    chip, core = dp // 2, lax.rem(dp, 2)
    mate = chip * 2 + (1 - core)
    base = 2 * rows
    steps = 2 * chunks

    def columns(c):
        return pl.ds(pl.multiple_of(c * width, width), width)

    def train_copy(c):
        return pltpu.make_async_copy(train_hbm.at[:, columns(c)], train.at[c], train_sem.at[c])

    def self_copy(c):
        return pltpu.make_async_copy(
            query_hbm.at[:, columns(c)], first_q.at[c, pl.ds(0, rows), :], self_sem.at[c]
        )

    def mate_copy(c):
        return pltpu.make_async_remote_copy(
            src_ref=query_hbm.at[:, columns(c)],
            dst_ref=first_q.at[c, pl.ds(rows, rows), :],
            send_sem=mate_send.at[c],
            recv_sem=mate_recv.at[c],
            device_id={"dp": mate},
        )

    def slot(group, c, place):
        if group == 0:
            return first_q.at[c, pl.ds(base + unit * place, unit), :]
        return second_q.at[c, pl.ds(unit * place, unit), :]

    def x_copy(group, c, d):
        start = pl.multiple_of(lax.rem(group + core, 2) * unit, unit)
        return pltpu.make_async_remote_copy(
            src_ref=query_hbm.at[pl.ds(start, unit), columns(c)],
            dst_ref=slot(group, c, 2 * (d - 1)),
            send_sem=x_send.at[d - 1, group * chunks + c],
            recv_sem=x_recv.at[d - 1, group * chunks + c],
            device_id={"dp": lax.rem(chip + d, chips) * 2 + core},
        )

    def fwd_copy(group, c, d):
        return pltpu.make_async_remote_copy(
            src_ref=slot(group, c, 2 * (d - 1)),
            dst_ref=slot(group, c, 2 * (d - 1) + 1),
            send_sem=fwd_send.at[d - 1, group * chunks + c],
            recv_sem=fwd_recv.at[d - 1, group * chunks + c],
            device_id={"dp": mate},
        )

    def pump(group, c):
        for d in range(1, chips):
            x_copy(group, c, d).wait_recv()
            fwd_copy(group, c, d).start()

    def piece_list(group):
        out = []
        if group == 0:
            for source, at in ((dp, 0), (mate, rows)):
                for r in range(0, rows, piece):
                    out.append((first_sum, at + r, source * rows + r))
        for d in range(1, chips):
            other = lax.rem(chip - d + chips, chips)
            for k in range(2):
                from_core = core if k == 0 else 1 - core
                start = lax.rem(group + from_core, 2) * unit
                at = unit * (2 * (d - 1) + k)
                for r in range(0, unit, piece):
                    row = (other * 2 + from_core) * rows + start + r
                    if group == 0:
                        out.append((first_sum, base + at + r, row))
                    else:
                        out.append((second_sum, at + r, row))
        return out

    first_pieces, second_pieces = piece_list(0), piece_list(1)

    def part_copy(index, item):
        buffer, at, row = item
        owner, offset = row // owned, lax.rem(row, owned)
        return owner, offset, pltpu.make_async_remote_copy(
            src_ref=buffer.at[pl.ds(at, piece), :],
            dst_ref=parts.at[me, pl.ds(pl.multiple_of(offset, piece), piece), :],
            send_sem=part_send.at[index],
            recv_sem=part_recv.at[me, offset // piece],
            device_id={"param": owner},
        )

    def send_parts(first_index, items):
        for i, item in enumerate(items):
            owner, offset, copy = part_copy(first_index + i, item)

            @pl.when(owner != me)
            def _():
                copy.start()

            @pl.when(owner == me)
            def _():
                buffer, at, _row = item
                parts[me, pl.ds(pl.multiple_of(offset, piece), piece), :] = buffer[pl.ds(at, piece), :]

    def wait_parts_sent(first_index, items):
        for i, item in enumerate(items):
            owner, _offset, copy = part_copy(first_index + i, item)

            @pl.when(owner != me)
            def _():
                copy.wait_send()

    def norm_copy(j):
        return pltpu.make_async_remote_copy(
            src_ref=norm_parts.at[me],
            dst_ref=norm_parts.at[me],
            send_sem=norm_send.at[j],
            recv_sem=norm_recv.at[me],
            device_id={"param": lax.rem(me + j, params)},
        )

    @pl.loop(0, chunks)
    def _(c):
        train_copy(c).start()
        self_copy(c).start()

    barrier = pltpu.get_barrier_semaphore()
    pl.semaphore_signal(barrier, inc=1, device_id={"dp": mate})
    for d in range(1, chips):
        pl.semaphore_signal(barrier, inc=1, device_id={"dp": lax.rem(chip + d, chips) * 2 + core})
    for j in range(1, params):
        pl.semaphore_signal(barrier, inc=1, device_id={"param": lax.rem(me + j, params)})
    pl.semaphore_wait(barrier, chips + params - 1)

    @pl.loop(0, chunks)
    def _(c):
        for d in range(1, chips):
            x_copy(0, c, d).start()
        mate_copy(c).start()

    @pl.loop(0, chunks)
    def _(c):
        for d in range(1, chips):
            x_copy(1, c, d).start()

    first_sum[...] = jnp.zeros_like(first_sum)
    second_sum[...] = jnp.zeros_like(second_sum)
    norm_sum[...] = jnp.zeros_like(norm_sum)

    def add_query_norm(total, q):
        acc = total[:, pl.ds(count, lanes)]
        for k in range(0, width, lanes):
            x = q[:, k : k + lanes].astype(jnp.float32)
            acc = acc + x * x
        total[:, pl.ds(count, lanes)] = acc

    for c in range(ahead):
        pump(0, c)

    @pl.loop(0, chunks)
    def _(c):
        @pl.when(c + ahead < chunks)
        def _():
            pump(0, c + ahead)

        @pl.when(c + ahead >= chunks)
        def _():
            pump(1, c + ahead - chunks)

        train_copy(c).wait()
        self_copy(c).wait()
        mate_copy(c).wait_recv()
        for d in range(1, chips):
            fwd_copy(0, c, d).wait_recv()
        q = first_q[c]
        add_query_norm(first_sum, q)
        for r in range(0, count, block_rows):
            size = min(block_rows, count - r)
            t = train[c, pl.ds(r, size), :]
            first_sum[:, pl.ds(r, size)] += nt_dot(q, t)
            for s in range(0, size, lanes):
                acc = norm_sum[pl.ds(r + s, lanes), :]
                for k in range(0, width, lanes):
                    x = t[s : s + lanes, k : k + lanes].astype(jnp.float32)
                    acc = acc + x * x
                norm_sum[pl.ds(r + s, lanes), :] = acc

    totals = [
        jnp.sum(norm_sum[pl.ds(r, lanes), :].T, axis=0, keepdims=True) for r in range(0, count, lanes)
    ]
    spare = norm_parts.shape[1] - len(totals)
    if spare:
        totals.append(jnp.zeros((spare, lanes), jnp.float32))
    norm_parts[me] = jnp.concatenate(totals, axis=0)
    send_parts(0, first_pieces)
    for j in range(1, params):
        norm_copy(j).start()

    @pl.loop(0, chunks)
    def _(c):
        @pl.when(c + ahead < chunks)
        def _():
            pump(1, c + ahead)

        for d in range(1, chips):
            fwd_copy(1, c, d).wait_recv()
        q = second_q[c]
        add_query_norm(second_sum, q)
        for r in range(0, count, block_rows):
            size = min(block_rows, count - r)
            second_sum[:, pl.ds(r, size)] += nt_dot(q, train[c, pl.ds(r, size), :])

    send_parts(len(first_pieces), second_pieces)

    @pl.loop(0, chunks)
    def _(c):
        mate_copy(c).wait_send()
        for d in range(1, chips):
            for group in range(2):
                x_copy(group, c, d).wait_send()
                fwd_copy(group, c, d).wait_send()

    norm = norm_parts[me]
    for j in range(1, params):
        other = lax.rem(me + j, params)
        pltpu.make_async_copy(norm_parts.at[other], norm_parts.at[other], norm_recv.at[other]).wait()
        norm = norm + norm_parts[other]
        norm_copy(j).wait_send()
    train_scale = lax.rsqrt(norm + epsilon)

    total = parts[me]
    for j in range(1, params):
        other = lax.rem(me + j, params)
        for k in range(owned // piece):
            place = parts.at[other, pl.ds(k * piece, piece), :]
            pltpu.make_async_copy(place, place, part_recv.at[other, k]).wait()
        total = total + parts[other]
    query_norm = jnp.sum(total[:, count:], axis=1, keepdims=True)
    query_scale = lax.rsqrt(query_norm + epsilon)
    for k in range(count // lanes):
        at = slice(k * lanes, (k + 1) * lanes)
        out_ref[:, at] = total[:, at] * query_scale * train_scale[k : k + 1, :]

    wait_parts_sent(0, first_pieces)
    wait_parts_sent(len(first_pieces), second_pieces)


def solution(mesh):
    chips, params = mesh.shape["dp"] // 2, mesh.shape["param"]

    def per_device(train_grads, query_grads):
        count, total = train_grads.shape
        rows = query_grads.shape[0]
        width = chunk_width(total)
        chunks = total // width
        unit = rows // 2
        owned = rows * chips * 2 // params
        piece = min(unit, owned)
        far = 2 * (chips - 1) * unit
        pieces = (2 * rows + 2 * far) // piece
        cfg = (chips, params, chunks, width, rows, unit, count, owned, piece)
        dma = pltpu.SemaphoreType.DMA
        return pl.pallas_call(
            functools.partial(kernel, cfg),
            out_shape=jax.ShapeDtypeStruct((owned, count), jnp.float32),
            in_specs=[pl.BlockSpec(memory_space=pl.ANY)] * 2,
            out_specs=pl.BlockSpec(memory_space=pltpu.VMEM),
            scratch_shapes=[
                pltpu.VMEM((chunks, count, width), jnp.bfloat16),
                pltpu.VMEM((chunks, 2 * rows + far, width), jnp.bfloat16),
                pltpu.VMEM((chunks, far, width), jnp.bfloat16),
                pltpu.VMEM((2 * rows + far, count + lanes), jnp.float32),
                pltpu.VMEM((far, count + lanes), jnp.float32),
                pltpu.VMEM((count, lanes), jnp.float32),
                pltpu.VMEM((params, owned, count + lanes), jnp.float32),
                pltpu.VMEM((params, -(-count // lanes // 8) * 8, lanes), jnp.float32),
                dma((chunks,)),
                dma((chunks,)),
                dma((chips - 1, 2 * chunks)),
                dma((chips - 1, 2 * chunks)),
                dma((chunks,)),
                dma((chunks,)),
                dma((chips - 1, 2 * chunks)),
                dma((chips - 1, 2 * chunks)),
                dma((pieces,)),
                dma((params, owned // piece)),
                dma((params,)),
                dma((params,)),
            ],
            compiler_params=pltpu.CompilerParams(
                collective_id=0, has_side_effects=True, vmem_limit_bytes=62 * 1024 * 1024
            ),
        )(train_grads, query_grads)

    return jax.shard_map(
        per_device,
        mesh=mesh,
        in_specs=(P("dp", "param"), P("dp", "param")),
        out_specs=P("param", "dp"),
        check_vma=False,
    )
```

time: 155 us -> 56.4 us (0.36); the launches traced: 153 us -> 56.3 us
  waiting for transfers between devices: 75.3 us -> 0 us
  Pallas kernels: 0 us -> 54.8 us
  matrix products: 22.4 us -> 0 us
  other arithmetic: 22.3 us -> 0 us
  blocking collectives: 18 us -> 0 us
  between operations: 14.1 us -> 0.01 us
    pallas_call x0 -> x1, Pallas kernels: none -> 54.8 us  [per_device(): pl.pallas_call(functools.partial(kernel, cfg), out_shape=jax.ShapeDtypeSt...]
    all_gather x1 -> x0, waiting for transfers between devices: 51.2 us -> none  [per_device(): queries = lax.all_gather(query_grads, 'dp', axis=0, tiled=True)]
    reduce_scatter x1 -> x0, waiting for transfers between devices: 23.4 us -> none  [per_device(): lax.psum_scatter(products, 'param', scatter_dimension=0, tiled=True)]
    dot_general x1 -> x0, matrix products: 22.4 us -> none  [per_device(): lax.dot_general(queries, train_grads, (((1,), (1,)), ((), ())), preferred...]
    reduce_sum x2 -> x0, other arithmetic: 20.7 us -> none  [the longest x1 16.4 us: per_device(): train_norm = jnp.sum(jnp.square(train_grads.astype(jnp.float32)), axis=1)]
    psum x1 -> x0, blocking collectives: 18 us -> none  [per_device(): train_norm = lax.psum(train_norm, 'param')]
  transfers between devices with their start and end apart: 2 -> 0, of which waited for: 2 -> 0; matrix products, arithmetic and copies ran while one was open for 14% -> 0% of each run, Pallas kernels for 0% -> 0%
where the time goes in v1:
time: 56.4 us; the launch traced here: 56.3 us
  Pallas kernels  54.8 us (97%)
  local copies, waits for them, and re-layouts  1.45 us (3%)
    pallas_call x1, Pallas kernels, per_device(): pl.pallas_call(functools.partial(kernel, cfg), out_shape=jax.ShapeDtypeSt...  54.8 us
    unnamed x1, local copies, waits for them, and re-layouts  1.45 us

profile of v1, /device:TPU:6, one launch (start us, length us, event | category | flops | bytes accessed | tf_op | source)
XLA Modules:
  0.0 56.3 jit_solution(8115621115052765514)
XLA Ops:
  0.0 54.8 %shard_map.28 = f32[16,896]{1,0:T(8,128)} custom-call(bf16[896,26624]{1,0:T(8,128)(2,1)} %train_hbm.1, bf16[32,26624]{1,0:T(8,128)(2,1)} %query_hbm.1), custom_call_target="tpu_custom_call" | custom-call | tf_op jit(solution)/shard_map/pallas_call | solution.py:296
  54.8 1.4 %copy.4 = f32[16,896]{1,0:T(8,128)} copy(f32[16,896]{1,0:T(8,128)} %shard_map.28) | data formatting | bytes 114688
